TPU v7x, 32 devices: a whole 2x2x4 slice. The times are simulated.
32 devices in a mesh: lat: 4 (over z), lon: 4 (over y, x), obs: 2 (over core).
Axes of the slice: x: 2, y: 2, z: 4, core: 2. Of those that a mesh axis runs over, the one named last changes fastest.
Arguments:
- innovation: float32 [4096, 128], P(('lat', 'lon', 'obs')), may hold values from -6 to 6
- obs_error: float32 [4096, 128], P(('lat', 'lon', 'obs')), may hold values from 0.5 to 2
- obs_offset: float32 [2, 4096, 128], P(None, ('lat', 'lon', 'obs')), may hold values from 0 to 1
- obs_cell: int32 [4096, 128], P(('lat', 'lon', 'obs')), may hold values from 0 to 65535
- obs_owner: int32 [32, 128], P(('lat', 'lon', 'obs')), may hold values from 0 to 15, as said below
- block_count: int32 [32], P(('lat', 'lon', 'obs')), may hold values from 64 to 128
- land_mask: int32 [256, 4096], P(('lat', 'obs'), 'lon'), may hold values from 0 to 1, as said below
- inertia: float32 [256, 4096], P(('lat', 'obs'), 'lon'), may hold values from 0.002 to 0.05
- sea_depth: float32 [256, 4096], P(('lat', 'obs'), 'lon'), may hold values from 0.5 to 5
Outputs:
- adjoint_field: float32 [256, 4096], P(('lat', 'obs'), 'lon')
- residual: float32 [256, 4096], P(('lat', 'obs'), 'lon')
Inputs may be any that keep to these rules, and one draw needn't show every extreme that they name: `obs_owner`: among the live blocks of one device at most 16 name the same tile; in every draw some tile is named by exactly 16 live blocks of every device. `land_mask`: the first and the last grid row are land.
All inputs are finite; a program needn't handle non-finite values.
Results may differ from a plain program's by a relative error of at most 0.0003.
Values sent between devices are 32-bit elements; how exact they have to be, the bound alone decides.
A program may use at most 64 MiB of HBM per device.

v0:
```python
import jax
import jax.numpy as jnp
from jax import lax
from jax.sharding import PartitionSpec as P

ITERS = 5


def extended(block, sides, width):
    for axis, dim in sides:
        count = lax.axis_size(axis)
        forward = [(i, i + 1) for i in range(count - 1)]
        forward.append((count - 1, 0))
        backward = [(target, source) for source, target in forward]
        low = lax.ppermute(
            lax.slice_in_dim(block, block.shape[dim] - width, None, axis=dim), axis, forward
        )
        high = lax.ppermute(lax.slice_in_dim(block, 0, width, axis=dim), axis, backward)
        block = jnp.concatenate([low, block, high], axis=dim)
    return block


def shifted(value, axis, steps):
    count = lax.axis_size(axis)
    pairs = [(source, (source + steps) % count) for source in range(count)]
    return lax.ppermute(value, axis, pairs)


def shifted_2(block, axis, distance):
    devices = range(lax.axis_size(axis))
    route = [(i - distance, i) for i in devices if i - distance in devices]
    return lax.ppermute(block, axis, route)


def border(field):
    return extended(field, ((("lat", "obs"), 0), ("lon", 1)), 1)


def two_products(residual, applied):
    return lax.psum(
        (jnp.sum(residual * residual), jnp.sum(residual * applied)), ("lat", "lon", "obs")
    )


def body(
    innovation,
    obs_error,
    obs_offset,
    obs_cell,
    obs_owner,
    block_count,
    land_mask,
    inertia,
    sea_depth,
):
    block_total = obs_owner.shape[1]
    block_width = innovation.shape[1]
    n_lat = lax.axis_size("lat")
    n_lon = lax.axis_size("lon")
    tile_count = n_lat * n_lon
    capacity = max(3, 2 * ((block_total + tile_count - 1) // tile_count))
    slot_total = tile_count * capacity
    tile_rows = land_mask.shape[0] * lax.axis_size("obs")
    tile_cols = land_mask.shape[1]
    owners = obs_owner[0]
    block_ids = jnp.arange(block_total)
    is_live = block_ids < block_count[0]
    earlier = block_ids[None, :] < block_ids[:, None]
    same_owner = (owners[None, :] == owners[:, None]) & earlier & is_live[None, :]
    slot_rank = jnp.sum(same_owner.astype(jnp.int32), axis=1)
    target = jnp.where(is_live, owners * capacity + slot_rank, slot_total)
    scaled = innovation / (obs_error * obs_error)
    floats = jnp.stack([scaled, obs_offset[0], obs_offset[1]], axis=1)

    def put_slots(values):
        holder = jnp.zeros((slot_total + 1,) + values.shape[1:], values.dtype)
        return holder.at[target].set(values)[:slot_total]

    sent_floats = put_slots(floats)
    sent_cells = put_slots(obs_cell)
    received, cell_ids = (
        lax.all_to_all(
            sent_floats.reshape(tile_count, capacity, 3, block_width),
            ("lat", "lon"),
            split_axis=0,
            concat_axis=0,
            tiled=True,
        ),
        lax.all_to_all(
            sent_cells.reshape(tile_count, capacity, block_width),
            ("lat", "lon"),
            split_axis=0,
            concat_axis=0,
            tiled=True,
        ),
    )
    received = received.reshape(-1, 3, block_width)
    cell_ids = cell_ids.reshape(-1, block_width)
    group = 1
    for size_try in range(1, slot_total + 1):
        if slot_total % size_try == 0 and size_try * block_width <= 4096:
            group = size_try
    turns = slot_total // group
    group_obs = group * block_width
    scaled_in = received[:, 0].reshape(turns, group_obs)
    north_frac = received[:, 1].reshape(turns, group_obs)
    east_frac = received[:, 2].reshape(turns, group_obs)
    cells_in = cell_ids.reshape(turns, group_obs)
    wide = tile_cols + 1
    row_axis = jnp.arange(tile_rows + 1, dtype=jnp.int32)[:, None]
    col_axis = jnp.arange(wide, dtype=jnp.int32)[None, :]

    def spread(total, pieces):
        amount, north, east, cells = pieces
        cell_row = (cells // tile_cols)[None, :]
        cell_col = (cells % tile_cols)[:, None]
        row_weights = (
            jnp.where(row_axis == cell_row, 1.0 - north[None, :], 0.0)
            + jnp.where(row_axis == cell_row + 1, north[None, :], 0.0)
        ) * amount[None, :]
        col_weights = jnp.where(col_axis == cell_col, 1.0 - east[:, None], 0.0) + jnp.where(
            col_axis == cell_col + 1, east[:, None], 0.0
        )
        return (
            total
            + jnp.dot(
                row_weights,
                col_weights,
                precision=lax.Precision.HIGHEST,
                preferred_element_type=jnp.float32,
            ),
            None,
        )

    partial_value, unused = lax.scan(
        spread,
        jnp.zeros((tile_rows + 1, wide), jnp.float32),
        (scaled_in, north_frac, east_frac, cells_in),
    )
    arrived_col = shifted(partial_value[:, tile_cols], "lon", 1)
    partial_value = partial_value[:, :tile_cols].at[:, 0].add(arrived_col)
    arrived_row = shifted_2(partial_value[tile_rows], "lat", 1)
    tile_part = partial_value[:tile_rows].at[0].add(arrived_row)
    ocean = land_mask.astype(jnp.float32)
    forcing = lax.psum_scatter(tile_part, "obs", scatter_dimension=0, tiled=True) * ocean
    conduct = ocean * sea_depth
    padded = border(conduct)
    cond_north = jnp.sqrt(conduct * padded[:-2, 1:-1])
    cond_south = jnp.sqrt(conduct * padded[2:, 1:-1])
    cond_west = jnp.sqrt(conduct * padded[1:-1, :-2])
    cond_east = jnp.sqrt(conduct * padded[1:-1, 2:])
    diagonal = inertia + cond_north + cond_south + cond_west + cond_east

    def operate(field):
        outer = border(field)
        return (
            diagonal * field
            - cond_north * outer[:-2, 1:-1]
            - cond_south * outer[2:, 1:-1]
            - cond_west * outer[1:-1, :-2]
            - cond_east * outer[1:-1, 2:]
        )

    adjoint_field = jnp.zeros_like(forcing)
    residual = forcing
    applied = operate(residual)
    norm_now, product = two_products(residual, applied)
    step_size = norm_now / product
    direction = residual
    applied_dir = applied
    for iteration in range(ITERS):
        adjoint_field = adjoint_field + step_size * direction
        residual = residual - step_size * applied_dir
        if iteration + 1 < ITERS:
            applied = operate(residual)
            norm_next, product = two_products(residual, applied)
            beta_ratio = norm_next / norm_now
            step_size = norm_next / (product - beta_ratio * norm_next / step_size)
            direction = residual + beta_ratio * direction
            applied_dir = applied + beta_ratio * applied_dir
            norm_now = norm_next
    return (adjoint_field, residual)


def solution(mesh):
    in_specs = (
        P(("lat", "lon", "obs"), None),
        P(("lat", "lon", "obs"), None),
        P(None, ("lat", "lon", "obs"), None),
        P(("lat", "lon", "obs"), None),
        P(("lat", "lon", "obs"), None),
        P(("lat", "lon", "obs")),
        P(("lat", "obs"), "lon"),
        P(("lat", "obs"), "lon"),
        P(("lat", "obs"), "lon"),
    )
    out_specs = (P(("lat", "obs"), "lon"), P(("lat", "obs"), "lon"))
    return jax.shard_map(body, mesh=mesh, in_specs=in_specs, out_specs=out_specs, check_vma=False)
```

profile of v0, /device:TPU:0, one launch (start us, length us, event | category | flops | bytes accessed | tf_op | source)
XLA Modules:
  0.0 499.3 jit_solution(3898041280866517940)
XLA Ops:
  11.3 8.3 %all-to-all-start = ((s32[16,16,128]{2,1,0:T(8,128)}), s32[16,16,128]{2,1,0:T(8,128)S(1)}, u32[]{:S(2)}, u32[]{:S(2)}) async-start(s32[16,16,128]{2,1,0:T(8,128)} %bitcast.5), calls=%async_computation | async-start | bytes 262144 | tf_op jit(solution)/shard_map/all_to_all | solution.py:89
  20.0 4.3 scatter_fusion
  25.2 2.3 all-to-all-done
  27.5 4.6 all-to-all-start.1
  32.2 12.0 %all-to-all-done.1 = f32[16,16,3,128]{3,1,2,0:T(8,128)S(1)} async-done(((f32[16,16,3,128]{3,1,2,0:T(8,128)}), f32[16,16,3,128]{3,1,2,0:T(8,128)S(1)}, u32[]{:S(2)}, u32[]{:S(2)}) %all-to-all-start.1) | async-done | bytes 393248 | tf_op jit(solution)/shard_map/all_to_all | solution.py:82
  44.4 152.0 %while.16 = (s32[]{:T(128)}, f32[65,1025]{1,0:T(8,128)S(1)}, s32[8,4096]{1,0:T(8,128)S(1)}, f32[8,4096]{1,0:T(8,128)S(1)}, f32[8,4096]{1,0:T(8,128)S(1)}, /*index=5*/f32[8,4096]{1,0:T(8,128)S(1)}, s32[]{:T(128)}, s32[]{:T(128)}) while((s32[]{:T(128)}, f32[65,1025]{1,0:T(8,128)S(1)}, s32[8,4096]{1,0:T(8,128)S(1)}, ...), condition=%wide.region_4.5_spmd.clone.clone, body=%wide.region_3.4_spmd.clone.clone.sunk | while | flops 3297597440 | bytes 942707 | solution.py:135
  44.6 18.7 %fusion.98 = f32[65,1025]{1,0:T(8,128)S(1)} fusion(f32[4096]{0:T(1024)S(1)} %bitcast.58, s32[4096]{0:T(1024)S(1)} %get-tuple-element.312, f32[4096]{0:T(1024)S(1)} %broadcast_subtract_fusion.5, s32[4096]{0:T(1024)S(1)} %get-tuple-element.313, f32[4096]{0:T(1024)S(1)} %bitcast.63, f32[4096]{0:T(1024)S(1)} %bitcast.62, s32[4096]{0:T(1024)S(1)} %bitcast.64, ...), kind=kOutput, calls=%fused_computation.15.clone.1 | convolution fusion | flops 3297474560 | bytes 680457 | tf_op jit(solution)/shard_map/while/body/eval_jaxpr/dot_general | solution.py:126
  63.6 18.7 %fusion.98 = f32[65,1025]{1,0:T(8,128)S(1)} fusion(f32[4096]{0:T(1024)S(1)} %bitcast.58, s32[4096]{0:T(1024)S(1)} %get-tuple-element.312, f32[4096]{0:T(1024)S(1)} %broadcast_subtract_fusion.5, s32[4096]{0:T(1024)S(1)} %get-tuple-element.313, f32[4096]{0:T(1024)S(1)} %bitcast.63, f32[4096]{0:T(1024)S(1)} %bitcast.62, s32[4096]{0:T(1024)S(1)} %bitcast.64, ...), kind=kOutput, calls=%fused_computation.15.clone.1 | convolution fusion | flops 3297474560 | bytes 680457 | tf_op jit(solution)/shard_map/while/body/eval_jaxpr/dot_general | solution.py:126
  82.6 18.7 %fusion.98 = f32[65,1025]{1,0:T(8,128)S(1)} fusion(f32[4096]{0:T(1024)S(1)} %bitcast.58, s32[4096]{0:T(1024)S(1)} %get-tuple-element.312, f32[4096]{0:T(1024)S(1)} %broadcast_subtract_fusion.5, s32[4096]{0:T(1024)S(1)} %get-tuple-element.313, f32[4096]{0:T(1024)S(1)} %bitcast.63, f32[4096]{0:T(1024)S(1)} %bitcast.62, s32[4096]{0:T(1024)S(1)} %bitcast.64, ...), kind=kOutput, calls=%fused_computation.15.clone.1 | convolution fusion | flops 3297474560 | bytes 680457 | tf_op jit(solution)/shard_map/while/body/eval_jaxpr/dot_general | solution.py:126
  101.5 18.7 %fusion.98 = f32[65,1025]{1,0:T(8,128)S(1)} fusion(f32[4096]{0:T(1024)S(1)} %bitcast.58, s32[4096]{0:T(1024)S(1)} %get-tuple-element.312, f32[4096]{0:T(1024)S(1)} %broadcast_subtract_fusion.5, s32[4096]{0:T(1024)S(1)} %get-tuple-element.313, f32[4096]{0:T(1024)S(1)} %bitcast.63, f32[4096]{0:T(1024)S(1)} %bitcast.62, s32[4096]{0:T(1024)S(1)} %bitcast.64, ...), kind=kOutput, calls=%fused_computation.15.clone.1 | convolution fusion | flops 3297474560 | bytes 680457 | tf_op jit(solution)/shard_map/while/body/eval_jaxpr/dot_general | solution.py:126
  120.5 18.7 %fusion.98 = f32[65,1025]{1,0:T(8,128)S(1)} fusion(f32[4096]{0:T(1024)S(1)} %bitcast.58, s32[4096]{0:T(1024)S(1)} %get-tuple-element.312, f32[4096]{0:T(1024)S(1)} %broadcast_subtract_fusion.5, s32[4096]{0:T(1024)S(1)} %get-tuple-element.313, f32[4096]{0:T(1024)S(1)} %bitcast.63, f32[4096]{0:T(1024)S(1)} %bitcast.62, s32[4096]{0:T(1024)S(1)} %bitcast.64, ...), kind=kOutput, calls=%fused_computation.15.clone.1 | convolution fusion | flops 3297474560 | bytes 680457 | tf_op jit(solution)/shard_map/while/body/eval_jaxpr/dot_general | solution.py:126
  139.5 18.7 %fusion.98 = f32[65,1025]{1,0:T(8,128)S(1)} fusion(f32[4096]{0:T(1024)S(1)} %bitcast.58, s32[4096]{0:T(1024)S(1)} %get-tuple-element.312, f32[4096]{0:T(1024)S(1)} %broadcast_subtract_fusion.5, s32[4096]{0:T(1024)S(1)} %get-tuple-element.313, f32[4096]{0:T(1024)S(1)} %bitcast.63, f32[4096]{0:T(1024)S(1)} %bitcast.62, s32[4096]{0:T(1024)S(1)} %bitcast.64, ...), kind=kOutput, calls=%fused_computation.15.clone.1 | convolution fusion | flops 3297474560 | bytes 680457 | tf_op jit(solution)/shard_map/while/body/eval_jaxpr/dot_general | solution.py:126
  158.5 18.7 %fusion.98 = f32[65,1025]{1,0:T(8,128)S(1)} fusion(f32[4096]{0:T(1024)S(1)} %bitcast.58, s32[4096]{0:T(1024)S(1)} %get-tuple-element.312, f32[4096]{0:T(1024)S(1)} %broadcast_subtract_fusion.5, s32[4096]{0:T(1024)S(1)} %get-tuple-element.313, f32[4096]{0:T(1024)S(1)} %bitcast.63, f32[4096]{0:T(1024)S(1)} %bitcast.62, s32[4096]{0:T(1024)S(1)} %bitcast.64, ...), kind=kOutput, calls=%fused_computation.15.clone.1 | convolution fusion | flops 3297474560 | bytes 680457 | tf_op jit(solution)/shard_map/while/body/eval_jaxpr/dot_general | solution.py:126
  177.5 18.7 %fusion.98 = f32[65,1025]{1,0:T(8,128)S(1)} fusion(f32[4096]{0:T(1024)S(1)} %bitcast.58, s32[4096]{0:T(1024)S(1)} %get-tuple-element.312, f32[4096]{0:T(1024)S(1)} %broadcast_subtract_fusion.5, s32[4096]{0:T(1024)S(1)} %get-tuple-element.313, f32[4096]{0:T(1024)S(1)} %bitcast.63, f32[4096]{0:T(1024)S(1)} %bitcast.62, s32[4096]{0:T(1024)S(1)} %bitcast.64, ...), kind=kOutput, calls=%fused_computation.15.clone.1 | convolution fusion | flops 3297474560 | bytes 680457 | tf_op jit(solution)/shard_map/while/body/eval_jaxpr/dot_general | solution.py:126
  198.0 3.0 collective-permute-done
  202.0 3.0 collective-permute-start.1
  205.0 1.3 collective-permute-done.1
  207.2 7.1 %reduce-scatter.2.cloned.1.call-done = f32[32,1024]{1,0:T(8,128)} async-done(((f32[64,1024]{1,0:T(8,128)}), f32[32,1024]{1,0:T(8,128)}) %reduce-scatter.2.cloned.1.call-update) | async-done | bytes 131088 | tf_op jit(solution)/shard_map/reduce_scatter | solution.py:145
  215.4 3.4 collective-permute-start.3
  218.9 3.5 collective-permute-start.7
  222.5 1.7 collective-permute-start.4
  224.1 1.3 collective-permute-start.5
  226.3 2.2 collective-permute-start.9
  228.4 1.7 collective-permute-done.8
  231.5 38.2 %all-reduce.4 = (f32[]{:T(128)}, f32[]{:T(128)}) all-reduce(f32[]{:T(128)} %get-tuple-element.194, f32[]{:T(128)} %get-tuple-element.193), channel_id=1, replica_groups=mesh['lat'=4,'lon'=4,'obs'=2] {'lat','lon','obs'}, use_global_device_ids=true, to_apply=%region_8.9 | all-reduce | flops 2 | bytes 16 | tf_op jit(solution)/shard_map/psum | solution.py:40
  271.2 3.5 collective-permute-start.11
  274.7 1.3 collective-permute-done.10
  276.1 2.3 collective-permute-start.12
  278.4 1.3 collective-permute-start.13
  279.7 1.7 collective-permute-done.12
  283.4 39.4 %all-reduce.3 = (f32[]{:T(128)}, f32[]{:T(128)}) all-reduce(f32[]{:T(128)} %get-tuple-element.192, f32[]{:T(128)} %get-tuple-element.191), channel_id=1, replica_groups=mesh['lat'=4,'lon'=4,'obs'=2] {'lat','lon','obs'}, use_global_device_ids=true, to_apply=%region_12.13 | all-reduce | flops 2 | bytes 16 | tf_op jit(solution)/shard_map/psum | solution.py:40
  327.4 3.5 collective-permute-start.15
  330.9 1.3 collective-permute-done.14
  332.4 2.3 collective-permute-start.16
  334.6 1.5 collective-permute-start.17
  336.1 1.7 collective-permute-done.16
  339.3 38.6 %all-reduce.2 = (f32[]{:T(128)}, f32[]{:T(128)}) all-reduce(f32[]{:T(128)} %get-tuple-element.190, f32[]{:T(128)} %get-tuple-element.189), channel_id=1, replica_groups=mesh['lat'=4,'lon'=4,'obs'=2] {'lat','lon','obs'}, use_global_device_ids=true, to_apply=%region_16.17 | all-reduce | flops 2 | bytes 16 | tf_op jit(solution)/shard_map/psum | solution.py:40
  382.0 3.5 collective-permute-start.19
  385.5 1.3 collective-permute-done.18
  387.0 2.3 collective-permute-start.20
  390.1 1.7 collective-permute-done.20
  394.0 39.2 %all-reduce.1 = (f32[]{:T(128)}, f32[]{:T(128)}) all-reduce(f32[]{:T(128)} %get-tuple-element.188, f32[]{:T(128)} %get-tuple-element.187), channel_id=1, replica_groups=mesh['lat'=4,'lon'=4,'obs'=2] {'lat','lon','obs'}, use_global_device_ids=true, to_apply=%region_20.21 | all-reduce | flops 2 | bytes 16 | tf_op jit(solution)/shard_map/psum | solution.py:40
  437.2 3.5 collective-permute-start.23
  440.7 1.3 collective-permute-done.22
  442.1 2.3 collective-permute-start.24
  444.4 1.6 collective-permute-start.25
  446.0 1.7 collective-permute-done.24
  449.1 38.6 %all-reduce = (f32[]{:T(128)}, f32[]{:T(128)}) all-reduce(f32[]{:T(128)} %get-tuple-element.186, f32[]{:T(128)} %get-tuple-element.185), channel_id=1, replica_groups=mesh['lat'=4,'lon'=4,'obs'=2] {'lat','lon','obs'}, use_global_device_ids=true, to_apply=%region_24.25 | all-reduce | flops 2 | bytes 16 | tf_op jit(solution)/shard_map/psum | solution.py:40
  (133 shorter events, 22.6 us)
Async XLA Ops:
  7.2 12.5 %copy-start.4 = (f32[2,128,128]{2,1,0:T(8,128)S(1)}, f32[2,128,128]{2,1,0:T(8,128)}, u32[]{:S(2)}) copy-start(f32[2,128,128]{2,1,0:T(8,128)} %param.17) | copy-start | bytes 393220
  7.2 12.5 %copy-start.5 = (f32[128,128]{1,0:T(8,128)S(1)}, f32[128,128]{1,0:T(8,128)}, u32[]{:S(2)}) copy-start(f32[128,128]{1,0:T(8,128)} %param.15) | copy-start | bytes 196612
  7.2 12.5 %copy-start.6 = (f32[128,128]{1,0:T(8,128)S(1)}, f32[128,128]{1,0:T(8,128)}, u32[]{:S(2)}) copy-start(f32[128,128]{1,0:T(8,128)} %param.16) | copy-start | bytes 196612
  11.3 16.1 %all-to-all-start = ((s32[16,16,128]{2,1,0:T(8,128)}), s32[16,16,128]{2,1,0:T(8,128)S(1)}, u32[]{:S(2)}, u32[]{:S(2)}) async-start(s32[16,16,128]{2,1,0:T(8,128)} %bitcast.5), calls=%async_computation | async-start | bytes 262144 | tf_op jit(solution)/shard_map/all_to_all | solution.py:89
  27.5 16.7 %all-to-all-start.1 = ((f32[16,16,3,128]{3,1,2,0:T(8,128)}), f32[16,16,3,128]{3,1,2,0:T(8,128)S(1)}, u32[]{:S(2)}, u32[]{:S(2)}) async-start(f32[16,16,3,128]{3,1,2,0:T(8,128)} %copy.29), calls=%async_computation.1 | async-start | bytes 786432 | tf_op jit(solution)/shard_map/all_to_all | solution.py:82
  32.1 182.1 %reduce-scatter.2.cloned.1.call-start = ((), (), s32[]{:S(2)}) async-start(), calls=%async_computation.3 | async-start | bytes 393216 | tf_op jit(solution)/shard_map/reduce_scatter | solution.py:145
  196.5 4.5 collective-permute-start
  198.0 16.2 %copy-start.2 = (f32[32,1024]{1,0:T(8,128)S(1)}, f32[32,1024]{1,0:T(8,128)}, u32[]{:S(2)}) copy-start(f32[32,1024]{1,0:T(8,128)} %param.23) | copy-start | bytes 393220
  198.0 16.2 %copy-start.3 = (s32[32,1024]{1,0:T(8,128)S(1)}, s32[32,1024]{1,0:T(8,128)}, u32[]{:S(2)}) copy-start(s32[32,1024]{1,0:T(8,128)} %param.21) | copy-start | bytes 393220
  202.0 4.3 collective-permute-start.1
  206.4 0.7 copy-start.1
  207.1 23.5 %copy-start = (f32[32,1024]{1,0:T(8,128)S(1)}, f32[32,1024]{1,0:T(8,128)}, u32[]{:S(2)}) copy-start(f32[32,1024]{1,0:T(8,128)} %param.22) | copy-start | bytes 393220
  215.2 7.2 %collective-permute-start.2 = (f32[1,1024]{1,0:T(1,128)S(1)}, f32[1,1024]{1,0:T(1,128)S(1)}, u32[]{:S(2)}, u32[]{:S(2)}) collective-permute-start(f32[1,1024]{1,0:T(1,128)S(1)} %get-tuple-element.257), channel_id=1, source_target_pairs={{0,1},{1,8},{8,9},{9,16},{16,17},{17,24},{24,25},{25,0},{2,3},{3,1... | collective-permute-start | bytes 12296 | tf_op jit(solution)/shard_map/ppermute | solution.py:15
  215.4 7.0 %collective-permute-start.3 = (f32[1,1024]{1,0:T(1,128)S(1)}, f32[1,1024]{1,0:T(1,128)S(1)}, u32[]{:S(2)}, u32[]{:S(2)}) collective-permute-start(f32[1,1024]{1,0:T(1,128)S(1)} %get-tuple-element.258), channel_id=1, source_target_pairs={{1,0},{8,1},{9,8},{16,9},{17,16},{24,17},{25,24},{0,25},{3,2},{10,... | collective-permute-start | bytes 12296 | tf_op jit(solution)/shard_map/ppermute | solution.py:18
  218.8 6.6 %collective-permute-start.6 = (f32[1,1024]{1,0:T(1,128)S(1)}, f32[1,1024]{1,0:T(1,128)S(1)}, u32[]{:S(2)}, u32[]{:S(2)}) collective-permute-start(f32[1,1024]{1,0:T(1,128)S(1)} %get-tuple-element.261), channel_id=1, source_target_pairs={{0,1},{1,8},{8,9},{9,16},{16,17},{17,24},{24,25},{25,0},{2,3},{3,1... | collective-permute-start | bytes 12296 | tf_op jit(solution)/shard_map/ppermute | solution.py:15
  218.9 6.5 %collective-permute-start.7 = (f32[1,1024]{1,0:T(1,128)S(1)}, f32[1,1024]{1,0:T(1,128)S(1)}, u32[]{:S(2)}, u32[]{:S(2)}) collective-permute-start(f32[1,1024]{1,0:T(1,128)S(1)} %get-tuple-element.262), channel_id=1, source_target_pairs={{1,0},{8,1},{9,8},{16,9},{17,16},{24,17},{25,24},{0,25},{3,2},{10,... | collective-permute-start | bytes 12296 | tf_op jit(solution)/shard_map/ppermute | solution.py:18
  222.5 5.9 %collective-permute-start.4 = (f32[34,1]{1,0:T(8,128)S(1)}, f32[34,1]{1,0:T(8,128)S(1)}, u32[]{:S(2)}, u32[]{:S(2)}) collective-permute-start(f32[34,1]{1,0:T(8,128)S(1)} %get-tuple-element.243), channel_id=1, source_target_pairs={{0,2},{2,4},{4,6},{6,0},{1,3},{3,5},{5,7},{7,1},{8,10},{10,12},{12... | collective-permute-start | bytes 416 | tf_op jit(solution)/shard_map/ppermute | solution.py:15
  224.1 4.3 collective-permute-start.5
  225.5 4.7 collective-permute-start.8
  226.3 4.3 collective-permute-start.9
  271.1 4.9 collective-permute-start.10
  271.2 4.9 collective-permute-start.11
  276.1 5.3 %collective-permute-start.12 = (f32[34,1]{1,0:T(8,128)S(1)}, f32[34,1]{1,0:T(8,128)S(1)}, u32[]{:S(2)}, u32[]{:S(2)}) collective-permute-start(f32[34,1]{1,0:T(8,128)S(1)} %get-tuple-element.241), channel_id=1, source_target_pairs={{0,2},{2,4},{4,6},{6,0},{1,3},{3,5},{5,7},{7,1},{8,10},{10,12},{12... | collective-permute-start | bytes 416 | tf_op jit(solution)/shard_map/ppermute | solution.py:15
  278.4 4.0 collective-permute-start.13
  327.3 4.9 collective-permute-start.14
  327.4 4.9 collective-permute-start.15
  332.4 5.5 %collective-permute-start.16 = (f32[34,1]{1,0:T(8,128)S(1)}, f32[34,1]{1,0:T(8,128)S(1)}, u32[]{:S(2)}, u32[]{:S(2)}) collective-permute-start(f32[34,1]{1,0:T(8,128)S(1)} %get-tuple-element.239), channel_id=1, source_target_pairs={{0,2},{2,4},{4,6},{6,0},{1,3},{3,5},{5,7},{7,1},{8,10},{10,12},{12... | collective-permute-start | bytes 416 | tf_op jit(solution)/shard_map/ppermute | solution.py:15
  334.6 3.8 collective-permute-start.17
  381.9 4.9 collective-permute-start.18
  382.0 4.9 collective-permute-start.19
  387.0 4.8 collective-permute-start.20
  389.2 3.8 collective-permute-start.21
  437.1 4.9 collective-permute-start.22
  437.2 4.9 collective-permute-start.23
  442.1 5.6 %collective-permute-start.24 = (f32[34,1]{1,0:T(8,128)S(1)}, f32[34,1]{1,0:T(8,128)S(1)}, u32[]{:S(2)}, u32[]{:S(2)}) collective-permute-start(f32[34,1]{1,0:T(8,128)S(1)} %get-tuple-element.235), channel_id=1, source_target_pairs={{0,2},{2,4},{4,6},{6,0},{1,3},{3,5},{5,7},{7,1},{8,10},{10,12},{12... | collective-permute-start | bytes 416 | tf_op jit(solution)/shard_map/ppermute | solution.py:15
  444.4 3.8 collective-permute-start.25
Sparse Core Ops, SparseCore 0:
  207.3 6.9 reduce-scatter.1
where the time goes:
time: 501 us; the launch traced here: 499 us
  blocking collectives  194 us (39%)
  matrix products  150 us (30%)
  starting transfers between devices  58.3 us (12%)
  waiting for transfers between devices  43.2 us (9%)
  between operations  32.8 us (7%)
  other arithmetic  11.1 us (2%)
  local copies, waits for them, and re-layouts  9.1 us (2%)
    psum x5, blocking collectives, two_products(): lax.psum((jnp.sum(residual * residual), jnp.sum(residual * applied)), ('l...  194 us
    dot_general x8, matrix products, spread(): jnp.dot(row_weights, col_weights, precision=lax.Precision.HIGHEST, prefer...  150 us
    ppermute x12, starting transfers between devices, extended(): lax.ppermute(lax.slice_in_dim(block, 0, width, axis=dim), axis, backward)  29.6 us
    ppermute x12, waiting for transfers between devices, extended(): lax.ppermute(lax.slice_in_dim(block, block.shape[dim] - width, None, axis...  13.7 us
    ppermute x12, starting transfers between devices, extended(): lax.ppermute(lax.slice_in_dim(block, block.shape[dim] - width, None, axis...  12.1 us
    all_to_all x1, waiting for transfers between devices, body(): lax.all_to_all(sent_floats.reshape(tile_count, capacity, 3, block_width),...  12 us
  transfers between devices with their start and end apart: 29, of which 19 were waited for; matrix products, arithmetic and copies ran while one was open for 1% of the time, Pallas kernels for 0%

commit v1 on v0

v1 whole, which is shorter than its diff:
```python
import functools

import jax
import jax.numpy as jnp
from jax import lax
from jax.experimental import pallas as pl
from jax.experimental.pallas import tpu as pltpu
from jax.sharding import PartitionSpec as P

ITERS = 5
ROW_PAD = 8
COL_PAD = 128
MESH = pl.DeviceIdType.MESH
AXES = ("lat", "lon", "obs")


def spread_kernel(row_span, half, d_ref, out_ref, acc_ref):
    step = pl.program_id(0)
    rows_all = 2 * row_span
    amount = d_ref[0, 0]
    north = d_ref[0, 1]
    east = d_ref[0, 2]
    key = d_ref[0, 3]
    row_id = jnp.floor(key * (1.0 / half))
    col_id = key - row_id * half - (half // 2)
    upper = amount * (1.0 - north)
    lower = amount * north
    pairs = []
    for share in (1.0 - east, east):
        top, bottom = upper * share, lower * share
        top_high = top.astype(jnp.bfloat16).astype(jnp.float32)
        bottom_high = bottom.astype(jnp.bfloat16).astype(jnp.float32)
        pairs.append((top_high, bottom_high))
        pairs.append((top - top_high, bottom - bottom_high))

    def wide(values, slot, count):
        tile = jnp.broadcast_to(values[slot : slot + 1], (16, values.shape[1]))
        tile = tile.astype(jnp.bfloat16)
        return jnp.concatenate([tile] * (count // 16), axis=0)

    width = amount.shape[1]
    row_axis = lax.broadcasted_iota(jnp.int32, (rows_all, width), 0)
    row_axis = row_axis.astype(jnp.float32).astype(jnp.bfloat16)
    row_axis_low = lax.broadcasted_iota(jnp.int32, (rows_all, width), 0) - 1
    row_axis_low = row_axis_low.astype(jnp.float32).astype(jnp.bfloat16)
    col_axis = lax.broadcasted_iota(jnp.int32, (half, width), 0) - (half // 2)
    col_axis = col_axis.astype(jnp.float32).astype(jnp.bfloat16)
    zero = jnp.zeros((), jnp.bfloat16)
    one = jnp.ones((), jnp.bfloat16)
    left, right = [], []
    for slot in range(amount.shape[0]):
        ids = wide(row_id, slot, rows_all)
        is_top = row_axis == ids
        is_bottom = row_axis_low == ids
        planes = [
            jnp.where(
                is_top,
                wide(top, slot, rows_all),
                jnp.where(is_bottom, wide(bottom, slot, rows_all), zero),
            )
            for top, bottom in pairs
        ]
        left.append(jnp.concatenate(planes, axis=0))
        right.append(jnp.where(col_axis == wide(col_id, slot, half), one, zero))
    product = lax.dot_general(
        jnp.concatenate(left, axis=1),
        jnp.concatenate(right, axis=1),
        (((1,), (1,)), ((), ())),
        preferred_element_type=jnp.float32,
    )

    @pl.when(step == 0)
    def _():
        acc_ref[...] = product

    @pl.when(step > 0)
    def _():
        acc_ref[...] = acc_ref[...] + product

    @pl.when(step == pl.num_programs(0) - 1)
    def _():
        def plane(index):
            first = acc_ref[2 * index * rows_all : (2 * index + 1) * rows_all]
            first = first + acc_ref[(2 * index + 1) * rows_all : (2 * index + 2) * rows_all]
            return jnp.concatenate([first[:row_span], first[row_span:]], axis=1)

        moved = pltpu.roll(plane(1), 1, 1)
        col = lax.broadcasted_iota(jnp.int32, moved.shape, 1)
        out_ref[:, : 2 * half] = plane(0) + jnp.where(col > 0, moved, 0.0)
        out_ref[:, 2 * half :] = jnp.where(
            col[:, :COL_PAD] == 0, moved[:, :COL_PAD], 0.0
        )


def solve_kernel(
    t_ref, g_ref, x_ref, r_ref,
    pair_ref, win_ref, west_ref, east_ref, edge_ref, wide_ref,
    up_ref, down_ref, mid_ref, cwest_ref, ceast_ref,
    diag_ref, cn_ref, cs_ref, cw_ref, ce_ref, res_ref, app_ref, dir_ref, adir_ref, sol_ref,
    part_ref, slot_ref, send_sem, recv_sem, sum_send, sum_recv,
):
    n_lat, n_lon, n_obs = (lax.axis_size(name) for name in AXES)
    lat, lon, core = (lax.axis_index(name) for name in AXES)
    total = n_lat * n_lon * n_obs
    me = (lat * n_lon + lon) * n_obs + core
    rows, cols = x_ref.shape
    tall = rows + 2 * ROW_PAD
    keep = rows + ROW_PAD

    def place(flat):
        return (flat // (n_lon * n_obs), (flat // n_obs) % n_lon, flat % n_obs)

    barrier = pltpu.get_barrier_semaphore()

    def greet(k, carry):
        pl.semaphore_signal(
            barrier, inc=1, device_id=place(lax.rem(me + k, total)), device_id_type=MESH
        )
        return carry

    lax.fori_loop(1, total, greet, 0)
    pl.semaphore_wait(barrier, total - 1)

    def copy(index, source, target, device):
        return pltpu.make_async_remote_copy(
            src_ref=source,
            dst_ref=target,
            send_sem=send_sem.at[index],
            recv_sem=recv_sem.at[index],
            device_id=device,
            device_id_type=MESH,
        )

    ring = n_lat * n_obs
    line = lat * n_obs + core
    above = lax.rem(line + ring - 1, ring)
    below = lax.rem(line + 1, ring)
    west = lax.rem(lon + n_lon - 1, n_lon)
    east = lax.rem(lon + 1, n_lon)
    split = rows - ROW_PAD
    mine = pl.multiple_of(core * split, 8)
    theirs = pl.multiple_of((1 - core) * split, 8)
    swap = copy(0, t_ref.at[pl.ds(theirs, tall)], pair_ref, (lat, lon, 1 - core))
    to_below = copy(
        1, g_ref.at[:, pl.ds(rows - ROW_PAD, ROW_PAD)], up_ref, (below // n_obs, lon, below % n_obs)
    )
    to_above = copy(
        2, g_ref.at[:, pl.ds(0, ROW_PAD)], down_ref, (above // n_obs, lon, above % n_obs)
    )
    swap.start()
    to_below.start()
    to_above.start()
    to_below.wait()
    to_above.wait()
    mid_ref[:, :ROW_PAD] = up_ref[...]
    mid_ref[:, ROW_PAD:keep] = g_ref[...]
    mid_ref[:, keep:] = down_ref[...]
    c_east = copy(3, mid_ref.at[:, :, pl.ds(cols - COL_PAD, COL_PAD)], cwest_ref, (lat, east, core))
    c_west = copy(4, mid_ref.at[:, :, pl.ds(0, COL_PAD)], ceast_ref, (lat, west, core))
    c_east.start()
    c_west.start()
    swap.wait()
    win_ref[...] = t_ref[pl.ds(mine, tall)] + pair_ref[...]
    t_east = copy(
        5, win_ref.at[:, pl.ds(cols - COL_PAD, 2 * COL_PAD)], west_ref, (lat, east, core)
    )
    t_west = copy(6, win_ref.at[:, pl.ds(0, COL_PAD)], east_ref, (lat, west, core))
    t_east.start()
    t_west.start()
    t_east.wait()
    t_west.wait()
    wide_ref[:, :COL_PAD] = west_ref[:, :COL_PAD]
    wide_ref[:, COL_PAD : 2 * COL_PAD] = win_ref[:, :COL_PAD] + west_ref[:, COL_PAD:]
    wide_ref[:, 2 * COL_PAD : COL_PAD + cols] = win_ref[:, COL_PAD:cols]
    wide_ref[:, COL_PAD + cols :] = east_ref[...] + win_ref[:, cols:]
    side = lax.rem(lat + n_lat + 2 * core - 1, n_lat)
    t_rows = copy(
        7,
        wide_ref.at[pl.ds(pl.multiple_of(core * rows, 8), 2 * ROW_PAD)],
        edge_ref,
        (side, lon, 1 - core),
    )
    t_rows.start()
    c_east.wait()
    c_west.wait()

    def widened(index):
        return jnp.concatenate([cwest_ref[index], mid_ref[index], ceast_ref[index]], axis=1)

    def moved(value, axis, back):
        size = value.shape[axis]
        return pltpu.roll(value, size - 1 if back else 1, axis)

    conduct = widened(0)
    cn = jnp.sqrt(conduct * moved(conduct, 0, False))
    cs = jnp.sqrt(conduct * moved(conduct, 0, True))
    cw = jnp.sqrt(conduct * moved(conduct, 1, False))
    ce = jnp.sqrt(conduct * moved(conduct, 1, True))
    cn_ref[...] = cn
    cs_ref[...] = cs
    cw_ref[...] = cw
    ce_ref[...] = ce
    diag_ref[...] = widened(1) + cn + cs + cw + ce
    t_rows.wait()

    @pl.when(core == 0)
    def _():
        spill = jnp.where(lat > 0, 1.0, 0.0)
        res_ref[:ROW_PAD] = edge_ref[:ROW_PAD]
        res_ref[ROW_PAD : 2 * ROW_PAD] = wide_ref[:ROW_PAD] + edge_ref[ROW_PAD:] * spill
        res_ref[2 * ROW_PAD :] = wide_ref[ROW_PAD:keep]

    @pl.when(core == 1)
    def _():
        spill = jnp.where(lat < n_lat - 1, 1.0, 0.0)
        res_ref[:keep] = wide_ref[:keep]
        res_ref[keep:] = edge_ref[:ROW_PAD] + wide_ref[keep:] * spill

    ocean = jnp.where(widened(0) > 0.0, 1.0, 0.0)
    res_ref[...] = res_ref[...] * ocean

    def inner(value):
        return value[ROW_PAD:keep, COL_PAD : COL_PAD + cols]

    def fold(value):
        value = inner(value)
        out = value[:8]
        for start in range(8, rows, 8):
            out = out + value[start : start + 8]
        lanes = out[:, :COL_PAD]
        for start in range(COL_PAD, cols, COL_PAD):
            lanes = lanes + out[:, start : start + COL_PAD]
        return jnp.sum(lanes, axis=(0, 1), keepdims=True)

    lane = lax.broadcasted_iota(jnp.int32, (1, COL_PAD), 1)

    def operate():
        field = res_ref[...]
        applied = (
            diag_ref[...] * field
            - cn_ref[...] * moved(field, 0, False)
            - cs_ref[...] * moved(field, 0, True)
            - cw_ref[...] * moved(field, 1, False)
            - ce_ref[...] * moved(field, 1, True)
        )
        app_ref[...] = applied
        first, second = fold(field * field), fold(field * applied)
        return jnp.where(lane == 0, first, jnp.where(lane == 1, second, 0.0))

    def reduced(values, turn):
        slot_ref[turn, pl.ds(me, 1)] = values[None]
        part_ref[turn] = values

        def post(k, carry):
            pltpu.make_async_remote_copy(
                src_ref=part_ref.at[turn],
                dst_ref=slot_ref.at[turn, me],
                send_sem=sum_send.at[turn],
                recv_sem=sum_recv.at[turn],
                device_id=place(lax.rem(me + k, total)),
                device_id_type=MESH,
            ).start()
            return carry

        lax.fori_loop(1, total, post, 0)
        block = slot_ref.at[turn, pl.ds(0, total - 1)]
        pltpu.make_async_copy(block, block, sum_recv.at[turn]).wait()
        pltpu.make_async_copy(block, block, sum_send.at[turn]).wait()
        sums = jnp.sum(slot_ref[turn], axis=0)
        return sums[:, 0:1], sums[:, 1:2]

    norm_now, product = reduced(operate(), 0)
    step_size = norm_now / product
    dir_ref[...] = res_ref[...]
    adir_ref[...] = app_ref[...]
    for turn in range(ITERS):
        scaled = step_size * inner(dir_ref[...])
        sol_ref[...] = scaled if turn == 0 else sol_ref[...] + scaled
        res_ref[...] = res_ref[...] - step_size * adir_ref[...]
        if turn + 1 < ITERS:
            norm_next, product = reduced(operate(), turn + 1)
            ratio = norm_next / norm_now
            step_size = norm_next / (product - ratio * norm_next / step_size)
            dir_ref[...] = res_ref[...] + ratio * dir_ref[...]
            adir_ref[...] = app_ref[...] + ratio * adir_ref[...]
            norm_now = norm_next
    x_ref[...] = sol_ref[...]
    r_ref[...] = inner(res_ref[...])


def body(
    innovation, obs_error, obs_offset, obs_cell, obs_owner, block_count,
    land_mask, inertia, sea_depth,
):
    block_total = obs_owner.shape[1]
    block_width = innovation.shape[1]
    n_lat, n_lon, n_obs = (lax.axis_size(name) for name in AXES)
    tile_count = n_lat * n_lon
    capacity = max(3, 2 * ((block_total + tile_count - 1) // tile_count))
    rows, cols = land_mask.shape
    tile_rows = rows * n_obs
    half = cols // 2
    row_span = tile_rows + 8
    total = tile_count * n_obs
    owners = obs_owner[0]
    block_ids = jnp.arange(block_total)
    is_live = block_ids < block_count[0]
    earlier = block_ids[None, :] < block_ids[:, None]
    same_owner = (owners[None, :] == owners[:, None]) & earlier & is_live[None, :]
    slot_rank = jnp.sum(same_owner.astype(jnp.int32), axis=1)
    target = jnp.where(is_live, owners * capacity + slot_rank, tile_count * capacity)
    place = (jnp.arange(tile_count * capacity)[:, None] == target[None, :]).astype(jnp.float32)
    scaled = innovation / (obs_error * obs_error)
    cell_row, cell_col = obs_cell // cols, obs_cell % cols
    key = ((cell_col // half) * row_span + cell_row) * half + cell_col % half
    data = jnp.stack([scaled, obs_offset[0], obs_offset[1], key.astype(jnp.float32)], axis=1)
    sent = jnp.dot(
        place,
        data.reshape(block_total, 4 * block_width),
        precision=lax.Precision.HIGHEST,
        preferred_element_type=jnp.float32,
    )
    sent = sent.reshape(tile_count, capacity, 4, block_width).transpose(0, 2, 1, 3)
    received = lax.all_to_all(sent, ("lat", "lon"), split_axis=0, concat_axis=0, tiled=True)
    tile = pl.pallas_call(
        functools.partial(spread_kernel, row_span, half),
        grid=(tile_count,),
        in_specs=[pl.BlockSpec((1, 4, capacity, block_width), lambda i: (i, 0, 0, 0))],
        out_specs=pl.BlockSpec((row_span, cols + COL_PAD), lambda i: (0, 0)),
        out_shape=jax.ShapeDtypeStruct((row_span, cols + COL_PAD), jnp.float32),
        scratch_shapes=[pltpu.VMEM((8 * row_span, half), jnp.float32)],
        compiler_params=pltpu.CompilerParams(dimension_semantics=("arbitrary",)),
        name="spread",
    )(received)
    conduct = land_mask.astype(jnp.float32) * sea_depth
    ground = jnp.stack([conduct, inertia])
    tall, broad = rows + 2 * ROW_PAD, cols + 2 * COL_PAD
    vmem = lambda *shape: pltpu.VMEM(shape, jnp.float32)
    return pl.pallas_call(
        solve_kernel,
        out_shape=[jax.ShapeDtypeStruct((rows, cols), jnp.float32)] * 2,
        in_specs=[pl.BlockSpec(memory_space=pltpu.VMEM)] * 2,
        out_specs=[pl.BlockSpec(memory_space=pltpu.VMEM)] * 2,
        scratch_shapes=[
            vmem(tall, cols + COL_PAD),
            vmem(tall, cols + COL_PAD),
            vmem(tall, 2 * COL_PAD),
            vmem(tall, COL_PAD),
            vmem(2 * ROW_PAD, broad),
            vmem(tall, broad),
            vmem(2, ROW_PAD, cols),
            vmem(2, ROW_PAD, cols),
            vmem(2, tall, cols),
            vmem(2, tall, COL_PAD),
            vmem(2, tall, COL_PAD),
        ]
        + [vmem(tall, broad)] * 9
        + [
            vmem(rows, cols),
            vmem(ITERS, 1, COL_PAD),
            vmem(ITERS, total, 1, COL_PAD),
            pltpu.SemaphoreType.DMA((8,)),
            pltpu.SemaphoreType.DMA((8,)),
            pltpu.SemaphoreType.DMA((ITERS,)),
            pltpu.SemaphoreType.DMA((ITERS,)),
        ],
        compiler_params=pltpu.CompilerParams(collective_id=0, has_side_effects=True),
        name="solve",
    )(tile, ground)


def solution(mesh):
    spread = P(AXES, None)
    grid = P(("lat", "obs"), "lon")
    in_specs = (spread, spread, P(None, AXES, None), spread, spread, P(AXES), grid, grid, grid)
    return jax.shard_map(
        body, mesh=mesh, in_specs=in_specs, out_specs=(grid, grid), check_vma=False
    )
```

time: 501 us -> 104 us (0.21)
  blocking collectives: 194 us -> 0 us
  matrix products: 150 us -> 1.21 us
  Pallas kernels: 0 us -> 69.4 us
  starting transfers between devices: 58.3 us -> 8.47 us
  between operations: 32.8 us -> 1.43 us
  waiting for transfers between devices: 43.2 us -> 13.4 us
  other arithmetic: 11.1 us -> 1.09 us
    psum x5 -> x0, blocking collectives: 194 us -> none  [two_products(): lax.psum((jnp.sum(residual * residual), jnp.sum(residual * applied)), ('l...]
    dot_general x8 -> x1, matrix products: 150 us -> 1.21 us  [body(): jnp.dot(place, data.reshape(block_total, 4 * block_width), precision=lax....]
    pallas_call x0 -> x2, Pallas kernels: none -> 69.4 us  [the longest x1 42.9 us: body(): pl.pallas_call(solve_kernel, out_shape=[jax.ShapeDtypeStruct((rows, cols)...]
    ppermute x26 -> x0, starting transfers between devices: 45.3 us -> none  [the longest x12 29.6 us: extended(): lax.ppermute(lax.slice_in_dim(block, 0, width, axis=dim), axis, backward)]
    ppermute x26 -> x0, waiting for transfers between devices: 21.9 us -> none  [the longest x12 13.7 us: extended(): lax.ppermute(lax.slice_in_dim(block, block.shape[dim] - width, None, axis...]
    reduce_scatter x1 -> x0, waiting for transfers between devices: 7.07 us -> none  [body(): lax.psum_scatter(tile_part, 'obs', scatter_dimension=0, tiled=True) * ocean]
    unnamed x14 -> x25, local copies, waits for them, and re-layouts: 0.74 us -> 7.26 us
    scatter x2 -> x0, local copies, waits for them, and re-layouts: 5.51 us -> none  [put_slots(): return holder.at[target].set(values)[:slot_total]]
  transfers between devices with their start and end apart: 29 -> 1, of which waited for: 19 -> 1; matrix products, arithmetic and copies ran while one was open for 1% -> 1% of each run, Pallas kernels for 0% -> 0%
where the time goes in v1:
time: 104 us; the launch traced here: 103 us
  Pallas kernels  69.4 us (67%)
  waiting for transfers between devices  13.4 us (13%)
  starting transfers between devices  8.47 us (8%)
  local copies, waits for them, and re-layouts  8.14 us (8%)
  between operations  1.43 us (1%)
  matrix products  1.21 us (1%)
  other arithmetic  1.09 us (1%)
    pallas_call x1, Pallas kernels, body(): pl.pallas_call(solve_kernel, out_shape=[jax.ShapeDtypeStruct((rows, cols)...  42.9 us
    pallas_call x1, Pallas kernels, body(): pl.pallas_call(functools.partial(spread_kernel, row_span, half), grid=(ti...  26.4 us
    all_to_all x1, waiting for transfers between devices, body(): lax.all_to_all(sent, ('lat', 'lon'), split_axis=0, concat_axis=0, tiled=T...  13.4 us
    all_to_all x1, starting transfers between devices, body(): lax.all_to_all(sent, ('lat', 'lon'), split_axis=0, concat_axis=0, tiled=T...  8.47 us
    unnamed x25, local copies, waits for them, and re-layouts  7.26 us
  transfers between devices with their start and end apart: 1, of which 1 were waited for; matrix products, arithmetic and copies ran while one was open for 1% of the time, Pallas kernels for 0%

profile of v1, /device:TPU:0, one launch (start us, length us, event | category | flops | bytes accessed | tf_op | source)
XLA Modules:
  0.0 103.1 jit_solution(10009043473701536301)
XLA Ops:
  1.3 0.9 fusion.26
  2.2 0.1 copy.30
  2.3 0.0 copy-start.5
  2.3 0.1 copy.31
  2.4 0.7 copy-done.5
  3.1 0.0 copy-start.6
  3.1 0.1 copy.20
  3.2 0.7 copy-done.6
  4.0 0.0 copy-start.7
  4.0 0.1 copy.22
  4.1 0.7 copy-done.7
  4.8 0.1 copy.25
  4.9 0.1 fusion.13
  5.0 0.0 copy-start.8
  5.1 0.6 copy-done.8
  5.7 0.2 convert_reduce_fusion
  5.9 1.2 %convolution_bitcast_fusion = f32[16,4,16,128]{3,2,1,0:T(8,128)} fusion(f32[128,1,128]{0,2,1:T(8,128)S(1)} %fusion.13, f32[128,1,128]{0,2,1:T(8,128)S(1)} %bitcast.36, f32[128,1,128]{0,2,1:T(8,128)S(1)} %bitcast.35, f32[128,1,128]{0,2,1:T(8,128)S(1)} %divide_bitcast_fusion, s32[128]{0:T(128)S(1)} %fusion.24, s32[16,16]{1,0:T(8,128)S(1)} %multiply_add_fusion), kind=kOutput, calls=%fused_computation | convolution fusion | flops 201555968 | bytes 787968 | tf_op jit(solution)/shard_map/dot_general | solution.py:317
  7.1 0.0 copy-start.1
  7.1 0.0 copy-start.2
  7.1 8.5 %all-to-all-start = ((f32[16,4,16,128]{3,2,1,0:T(8,128)}), f32[16,4,16,128]{3,2,1,0:T(8,128)S(1)}, u32[]{:S(2)}, u32[]{:S(2)}) async-start(f32[16,4,16,128]{3,2,1,0:T(8,128)} %convolution_bitcast_fusion), calls=%async_computation | async-start | bytes 1048576 | tf_op jit(solution)/shard_map/all_to_all | solution.py:324
  15.6 0.0 copy-done.1
  15.6 0.0 copy-done.2
  15.6 0.0 copy-start.4
  15.7 0.9 copy-done.4
  16.5 0.7 pad_maximum_fusion.g_ref
  17.3 13.4 %all-to-all-done.d_ref = f32[16,4,16,128]{3,2,1,0:T(8,128)S(1)} async-done(((f32[16,4,16,128]{3,2,1,0:T(8,128)}), f32[16,4,16,128]{3,2,1,0:T(8,128)S(1)}, u32[]{:S(2)}, u32[]{:S(2)}) %all-to-all-start) | async-done | bytes 524320 | tf_op jit(solution)/shard_map/all_to_all | solution.py:324
  30.7 0.0 copy-start
  30.7 0.8 copy-done
  31.5 26.4 %spread.1.t_ref = f32[72,1152]{1,0:T(8,128)} custom-call(f32[16,4,16,128]{3,2,1,0:T(8,128)} %copy-done), custom_call_target="tpu_custom_call" | custom-call | tf_op jit(solution)/shard_map/spread/pallas_call | solution.py:325
  57.9 42.9 %solve.1 = (f32[32,1024]{1,0:T(8,128)}, f32[32,1024]{1,0:T(8,128)}) custom-call(f32[72,1152]{1,0:T(8,128)} %spread.1.t_ref, f32[2,32,1024]{2,1,0:T(8,128)} %pad_maximum_fusion.g_ref), custom_call_target="tpu_custom_call" | custom-call | tf_op jit(solution)/shard_map/solve/pallas_call | solution.py:339
  100.9 0.0 copy-start.3
  100.9 1.6 %copy.35 = f32[32,1024]{1,0:T(8,128)} copy(f32[32,1024]{1,0:T(8,128)} %get-tuple-element.6) | data formatting | bytes 262144
  102.5 0.0 copy-done.3
  102.5 0.7 copy.36
  (5 shorter events, 0.1 us)
Async XLA Ops:
  2.3 0.8 copy-start.5
  3.1 0.8 copy-start.6
  4.0 0.8 copy-start.7
  5.0 0.7 copy-start.8
  7.1 8.5 %copy-start.1 = (f32[32,1024]{1,0:T(8,128)S(1)}, f32[32,1024]{1,0:T(8,128)}, u32[]{:S(2)}) copy-start(f32[32,1024]{1,0:T(8,128)} %param.17) | copy-start | bytes 393220
  7.1 8.5 %copy-start.2 = (s32[32,1024]{1,0:T(8,128)S(1)}, s32[32,1024]{1,0:T(8,128)}, u32[]{:S(2)}) copy-start(s32[32,1024]{1,0:T(8,128)} %param.15) | copy-start | bytes 393220
  7.1 23.6 %all-to-all-start = ((f32[16,4,16,128]{3,2,1,0:T(8,128)}), f32[16,4,16,128]{3,2,1,0:T(8,128)S(1)}, u32[]{:S(2)}, u32[]{:S(2)}) async-start(f32[16,4,16,128]{3,2,1,0:T(8,128)} %convolution_bitcast_fusion), calls=%async_computation | async-start | bytes 1048576 | tf_op jit(solution)/shard_map/all_to_all | solution.py:324
  15.6 0.9 copy-start.4
  30.7 0.8 copy-start
  100.9 1.6 %copy-start.3 = (f32[32,1024]{1,0:T(8,128)S(1)}, f32[32,1024]{1,0:T(8,128)}, u32[]{:S(2)}) copy-start(f32[32,1024]{1,0:T(8,128)} %get-tuple-element.7) | copy-start | bytes 393220

commit v2 on v1

--- a/solution.py
+++ b/solution.py
@@ -8,19 +8,79 @@
 from jax.sharding import PartitionSpec as P
 
 ITERS = 5
+STAGES = (2, 2, 1)
 ROW_PAD = 8
 COL_PAD = 128
 MESH = pl.DeviceIdType.MESH
 AXES = ("lat", "lon", "obs")
 
 
-def spread_kernel(row_span, half, d_ref, out_ref, acc_ref):
-    step = pl.program_id(0)
+def spread_kernel(row_span, half, d_ref, out_ref, inbox_ref, acc_ref, send_sem, recv_sem):
+    n_lon = lax.axis_size("lon")
+    count = lax.axis_size("lat") * n_lon
+    core = lax.axis_index("obs")
+    me = lax.axis_index("lat") * n_lon + lax.axis_index("lon")
+    barrier = pltpu.get_barrier_semaphore()
+
+    def place(flat):
+        return (flat // n_lon, flat % n_lon, core)
+
+    def greet(k, carry):
+        pl.semaphore_signal(
+            barrier, inc=1, device_id=place(lax.rem(me + k, count)), device_id_type=MESH
+        )
+        return carry
+
+    def copy(k):
+        target = lax.rem(me + k, count)
+        return pltpu.make_async_remote_copy(
+            src_ref=d_ref.at[target],
+            dst_ref=inbox_ref.at[k],
+            send_sem=send_sem.at[k],
+            recv_sem=recv_sem.at[k],
+            device_id=place(target),
+            device_id_type=MESH,
+        )
+
+    def send(k, carry):
+        copy(k).start()
+        return carry
+
+    def finish(k, carry):
+        copy(k).wait_send()
+        return carry
+
+    lax.fori_loop(1, count, greet, 0)
+    pl.semaphore_wait(barrier, count - 1)
+    lax.fori_loop(1, count, send, 0)
+    acc_ref[...] = spread_block(row_span, half, d_ref[me])
+
+    def turn(k, carry):
+        copy(k).wait_recv()
+        acc_ref[...] = acc_ref[...] + spread_block(row_span, half, inbox_ref[k])
+        return carry
+
+    lax.fori_loop(1, count, turn, 0)
+    lax.fori_loop(1, count, finish, 0)
     rows_all = 2 * row_span
-    amount = d_ref[0, 0]
-    north = d_ref[0, 1]
-    east = d_ref[0, 2]
-    key = d_ref[0, 3]
+
+    def plane(index):
+        first = acc_ref[2 * index * rows_all : (2 * index + 1) * rows_all]
+        first = first + acc_ref[(2 * index + 1) * rows_all : (2 * index + 2) * rows_all]
+        return jnp.concatenate([first[:row_span], first[row_span:]], axis=1)
+
+    moved = pltpu.roll(plane(1), 1, 1)
+    col = lax.broadcasted_iota(jnp.int32, moved.shape, 1)
+    out_ref[:, : 2 * half] = plane(0) + jnp.where(col > 0, moved, 0.0)
+    out_ref[:, 2 * half :] = jnp.where(col[:, :COL_PAD] == 0, moved[:, :COL_PAD], 0.0)
+
+
+def spread_block(row_span, half, block):
+    rows_all = 2 * row_span
+    amount = block[0]
+    north = block[1]
+    east = block[2]
+    key = block[3]
     row_id = jnp.floor(key * (1.0 / half))
     col_id = key - row_id * half - (half // 2)
     upper = amount * (1.0 - north)
@@ -62,41 +122,19 @@
         ]
         left.append(jnp.concatenate(planes, axis=0))
         right.append(jnp.where(col_axis == wide(col_id, slot, half), one, zero))
-    product = lax.dot_general(
+    return lax.dot_general(
         jnp.concatenate(left, axis=1),
         jnp.concatenate(right, axis=1),
         (((1,), (1,)), ((), ())),
         preferred_element_type=jnp.float32,
     )
 
-    @pl.when(step == 0)
-    def _():
-        acc_ref[...] = product
-
-    @pl.when(step > 0)
-    def _():
-        acc_ref[...] = acc_ref[...] + product
-
-    @pl.when(step == pl.num_programs(0) - 1)
-    def _():
-        def plane(index):
-            first = acc_ref[2 * index * rows_all : (2 * index + 1) * rows_all]
-            first = first + acc_ref[(2 * index + 1) * rows_all : (2 * index + 2) * rows_all]
-            return jnp.concatenate([first[:row_span], first[row_span:]], axis=1)
-
-        moved = pltpu.roll(plane(1), 1, 1)
-        col = lax.broadcasted_iota(jnp.int32, moved.shape, 1)
-        out_ref[:, : 2 * half] = plane(0) + jnp.where(col > 0, moved, 0.0)
-        out_ref[:, 2 * half :] = jnp.where(
-            col[:, :COL_PAD] == 0, moved[:, :COL_PAD], 0.0
-        )
-
 
 def solve_kernel(
     t_ref, g_ref, x_ref, r_ref,
     pair_ref, win_ref, west_ref, east_ref, edge_ref, wide_ref,
     up_ref, down_ref, mid_ref, cwest_ref, ceast_ref,
-    diag_ref, cn_ref, cs_ref, cw_ref, ce_ref, res_ref, app_ref, dir_ref, adir_ref, sol_ref,
+    diag_ref, cn_ref, cs_ref, cw_ref, ce_ref, res_ref, app_ref, dir_ref, adir_ref, far_ref, sol_ref,
     part_ref, slot_ref, send_sem, recv_sem, sum_send, sum_recv,
 ):
     n_lat, n_lon, n_obs = (lax.axis_size(name) for name in AXES)
@@ -222,8 +260,8 @@
     def inner(value):
         return value[ROW_PAD:keep, COL_PAD : COL_PAD + cols]
 
-    def fold(value):
-        value = inner(value)
+    def fold(left, right):
+        value = inner(left) * inner(right)
         out = value[:8]
         for start in range(8, rows, 8):
             out = out + value[start : start + 8]
@@ -234,18 +272,15 @@
 
     lane = lax.broadcasted_iota(jnp.int32, (1, COL_PAD), 1)
 
-    def operate():
-        field = res_ref[...]
-        applied = (
+    def operate(source, target):
+        field = source[...]
+        target[...] = (
             diag_ref[...] * field
             - cn_ref[...] * moved(field, 0, False)
             - cs_ref[...] * moved(field, 0, True)
             - cw_ref[...] * moved(field, 1, False)
             - ce_ref[...] * moved(field, 1, True)
         )
-        app_ref[...] = applied
-        first, second = fold(field * field), fold(field * applied)
-        return jnp.where(lane == 0, first, jnp.where(lane == 1, second, 0.0))
 
     def reduced(values, turn):
         slot_ref[turn, pl.ds(me, 1)] = values[None]
@@ -266,24 +301,80 @@
         block = slot_ref.at[turn, pl.ds(0, total - 1)]
         pltpu.make_async_copy(block, block, sum_recv.at[turn]).wait()
         pltpu.make_async_copy(block, block, sum_send.at[turn]).wait()
-        sums = jnp.sum(slot_ref[turn], axis=0)
-        return sums[:, 0:1], sums[:, 1:2]
-
-    norm_now, product = reduced(operate(), 0)
-    step_size = norm_now / product
+        return jnp.sum(slot_ref[turn], axis=0)
+
+    def axpy(base, factor, extra):
+        out = []
+        for one, two in zip(base, extra):
+            if two is None:
+                out.append(one)
+            else:
+                out.append(factor * two if one is None else one + factor * two)
+        return out
+
+    unit = jnp.ones((1, 1), jnp.float32)
     dir_ref[...] = res_ref[...]
-    adir_ref[...] = app_ref[...]
-    for turn in range(ITERS):
-        scaled = step_size * inner(dir_ref[...])
-        sol_ref[...] = scaled if turn == 0 else sol_ref[...] + scaled
-        res_ref[...] = res_ref[...] - step_size * adir_ref[...]
-        if turn + 1 < ITERS:
-            norm_next, product = reduced(operate(), turn + 1)
-            ratio = norm_next / norm_now
-            step_size = norm_next / (product - ratio * norm_next / step_size)
-            dir_ref[...] = res_ref[...] + ratio * dir_ref[...]
-            adir_ref[...] = app_ref[...] + ratio * adir_ref[...]
-            norm_now = norm_next
+    done = 0
+    for turn, count in enumerate(STAGES):
+        along = [dir_ref, adir_ref, far_ref][: count + 1]
+        across = [] if turn == 0 else [res_ref, app_ref][:count]
+        for chain in (along, across):
+            for source, target in zip(chain[:-1], chain[1:]):
+                operate(source, target)
+        vectors = along + across
+        size = len(vectors)
+        fields = [ref[...] for ref in vectors]
+        pairs = [(i, j) for i in range(size) for j in range(i, size)]
+        values = jnp.zeros((1, COL_PAD), jnp.float32)
+        for number, (i, j) in enumerate(pairs):
+            values = jnp.where(lane == number, fold(fields[i], fields[j]), values)
+        sums = reduced(values, turn)
+        gram = {}
+        for number, (i, j) in enumerate(pairs):
+            gram[i, j] = gram[j, i] = sums[:, number : number + 1]
+
+        def quad(first, second):
+            out = None
+            for i in range(size):
+                row = None
+                for j in range(size):
+                    if second[j] is not None:
+                        term = second[j] * gram[i, j]
+                        row = term if row is None else row + term
+                if first[i] is not None:
+                    out = first[i] * row if out is None else out + first[i] * row
+            return out
+
+        direct = [unit] + [None] * (size - 1)
+        resid = [None] * size
+        resid[count + 1 if across else 0] = unit
+        gained = [None] * size
+        norm = quad(resid, resid)
+        for _ in range(count):
+            done += 1
+            applied = [None] + direct[:count]
+            if across:
+                applied += [None] + direct[count + 1 : size - 1]
+            step_size = norm / quad(direct, applied)
+            gained = axpy(gained, step_size, direct)
+            resid = axpy(resid, -step_size, applied)
+            if done < ITERS:
+                norm_next = quad(resid, resid)
+                direct = axpy(resid, norm_next / norm, direct)
+                norm = norm_next
+
+        def mix(weights, parts):
+            out = None
+            for weight, part in zip(weights, parts):
+                if weight is not None:
+                    out = weight * part if out is None else out + weight * part
+            return out
+
+        gain = mix(gained, [inner(field) for field in fields])
+        sol_ref[...] = gain if turn == 0 else sol_ref[...] + gain
+        res_ref[...] = mix(resid, fields)
+        if done < ITERS:
+            dir_ref[...] = mix(direct, fields)
     x_ref[...] = sol_ref[...]
     r_ref[...] = inner(res_ref[...])
 
@@ -321,17 +412,20 @@
         preferred_element_type=jnp.float32,
     )
     sent = sent.reshape(tile_count, capacity, 4, block_width).transpose(0, 2, 1, 3)
-    received = lax.all_to_all(sent, ("lat", "lon"), split_axis=0, concat_axis=0, tiled=True)
     tile = pl.pallas_call(
         functools.partial(spread_kernel, row_span, half),
-        grid=(tile_count,),
-        in_specs=[pl.BlockSpec((1, 4, capacity, block_width), lambda i: (i, 0, 0, 0))],
-        out_specs=pl.BlockSpec((row_span, cols + COL_PAD), lambda i: (0, 0)),
+        in_specs=[pl.BlockSpec(memory_space=pltpu.VMEM)],
+        out_specs=pl.BlockSpec(memory_space=pltpu.VMEM),
         out_shape=jax.ShapeDtypeStruct((row_span, cols + COL_PAD), jnp.float32),
-        scratch_shapes=[pltpu.VMEM((8 * row_span, half), jnp.float32)],
-        compiler_params=pltpu.CompilerParams(dimension_semantics=("arbitrary",)),
+        scratch_shapes=[
+            pltpu.VMEM((tile_count, 4, capacity, block_width), jnp.float32),
+            pltpu.VMEM((8 * row_span, half), jnp.float32),
+            pltpu.SemaphoreType.DMA((tile_count,)),
+            pltpu.SemaphoreType.DMA((tile_count,)),
+        ],
+        compiler_params=pltpu.CompilerParams(collective_id=1, has_side_effects=True),
         name="spread",
-    )(received)
+    )(sent)
     conduct = land_mask.astype(jnp.float32) * sea_depth
     ground = jnp.stack([conduct, inertia])
     tall, broad = rows + 2 * ROW_PAD, cols + 2 * COL_PAD
@@ -354,15 +448,15 @@
             vmem(2, tall, COL_PAD),
             vmem(2, tall, COL_PAD),
         ]
-        + [vmem(tall, broad)] * 9
+        + [vmem(tall, broad)] * 10
         + [
             vmem(rows, cols),
-            vmem(ITERS, 1, COL_PAD),
-            vmem(ITERS, total, 1, COL_PAD),
+            vmem(len(STAGES), 1, COL_PAD),
+            vmem(len(STAGES), total, 1, COL_PAD),
             pltpu.SemaphoreType.DMA((8,)),
             pltpu.SemaphoreType.DMA((8,)),
-            pltpu.SemaphoreType.DMA((ITERS,)),
-            pltpu.SemaphoreType.DMA((ITERS,)),
+            pltpu.SemaphoreType.DMA((len(STAGES),)),
+            pltpu.SemaphoreType.DMA((len(STAGES),)),
         ],
         compiler_params=pltpu.CompilerParams(collective_id=0, has_side_effects=True),
         name="solve",

time: 104 us -> 81.4 us (0.78)
  waiting for transfers between devices: 13.4 us -> 0 us
  starting transfers between devices: 8.47 us -> 0 us
    all_to_all x1 -> x0, waiting for transfers between devices: 13.4 us -> none  [body(): lax.all_to_all(sent, ('lat', 'lon'), split_axis=0, concat_axis=0, tiled=T...]
    all_to_all x1 -> x0, starting transfers between devices: 8.47 us -> none  [body(): lax.all_to_all(sent, ('lat', 'lon'), split_axis=0, concat_axis=0, tiled=T...]
    pallas_call x1, Pallas kernels: 26.4 us -> 34 us  [body(): pl.pallas_call(functools.partial(spread_kernel, row_span, half), in_specs...]
    pallas_call x1, Pallas kernels: 42.9 us -> 35.8 us  [body(): pl.pallas_call(solve_kernel, out_shape=[jax.ShapeDtypeStruct((rows, cols)...]
    unnamed x25 -> x23, local copies, waits for them, and re-layouts: 7.26 us -> 6.53 us
  transfers between devices with their start and end apart: 1 -> 0, of which waited for: 1 -> 0; matrix products, arithmetic and copies ran while one was open for 1% -> 0% of each run, Pallas kernels for 0% -> 0%
where the time goes in v2:
time: 81.4 us; the launch traced here: 81 us
  Pallas kernels  69.8 us (86%)
  local copies, waits for them, and re-layouts  7.42 us (9%)
  between operations  1.44 us (2%)
  matrix products  1.21 us (1%)
  other arithmetic  1.07 us (1%)
    pallas_call x1, Pallas kernels, body(): pl.pallas_call(solve_kernel, out_shape=[jax.ShapeDtypeStruct((rows, cols)...  35.8 us
    pallas_call x1, Pallas kernels, body(): pl.pallas_call(functools.partial(spread_kernel, row_span, half), in_specs...  34 us
    unnamed x23, local copies, waits for them, and re-layouts  6.53 us

profile of v2, /device:TPU:0, one launch (start us, length us, event | category | flops | bytes accessed | tf_op | source)
XLA Modules:
  0.0 81.0 jit_solution(3138573005531274743)
XLA Ops:
  1.3 0.0 copy-start.7
  1.3 0.6 copy-done.7
  1.9 0.2 convert_reduce_fusion
  2.1 0.9 %fusion.26 = (f32[1,128,128]{2,1,0:T(8,128)S(1)}, f32[1,128,128]{2,1,0:T(8,128)S(1)}) fusion(f32[2,128,128]{2,1,0:T(8,128)} %param.11), kind=kLoop, calls=%fused_computation.49 | loop fusion | bytes 262144 | tf_op jit(solution)/shard_map/slice | solution.py:407
  3.0 0.1 copy.30
  3.1 0.0 copy-start.4
  3.1 0.1 copy.31
  3.2 0.7 copy-done.4
  4.0 0.0 copy-start.5
  4.0 0.1 copy.20
  4.1 0.7 copy-done.5
  4.8 0.1 copy.22
  4.9 0.0 copy-start.6
  4.9 0.8 copy-done.6
  5.7 0.1 copy.25
  5.8 0.1 fusion.13
  6.0 1.2 %convolution_bitcast_fusion.d_ref = f32[16,4,16,128]{3,2,1,0:T(8,128)} fusion(f32[128,1,128]{0,2,1:T(8,128)S(1)} %fusion.13, f32[128,1,128]{0,2,1:T(8,128)S(1)} %bitcast.36, f32[128,1,128]{0,2,1:T(8,128)S(1)} %bitcast.35, f32[128,1,128]{0,2,1:T(8,128)S(1)} %divide_bitcast_fusion, s32[128]{0:T(128)S(1)} %fusion.24, s32[16,16]{1,0:T(8,128)S(1)} %multiply_add_fusion), kind=kOutput, calls=%fused_computation | convolution fusion | flops 201555968 | bytes 787968 | tf_op jit(solution)/shard_map/dot_general | solution.py:408
  7.2 0.0 copy-start
  7.2 0.0 copy-start.1
  7.2 34.0 %spread.1.t_ref = f32[72,1152]{1,0:T(8,128)} custom-call(f32[16,4,16,128]{3,2,1,0:T(8,128)} %convolution_bitcast_fusion.d_ref), custom_call_target="tpu_custom_call" | custom-call | tf_op jit(solution)/shard_map/spread/pallas_call | solution.py:415
  41.3 0.0 copy-done
  41.3 0.0 copy-done.1
  41.3 0.0 copy-start.3
  41.3 0.9 %copy-done.3 = f32[32,1024]{1,0:T(8,128)S(1)} copy-done((f32[32,1024]{1,0:T(8,128)S(1)}, f32[32,1024]{1,0:T(8,128)}, u32[]{:S(2)}) %copy-start.3) | copy-done | bytes 131096
  42.2 0.7 pad_maximum_fusion.g_ref
  42.9 35.8 %solve.1 = (f32[32,1024]{1,0:T(8,128)}, f32[32,1024]{1,0:T(8,128)}) custom-call(f32[72,1152]{1,0:T(8,128)} %spread.1.t_ref, f32[2,32,1024]{2,1,0:T(8,128)} %pad_maximum_fusion.g_ref), custom_call_target="tpu_custom_call" | custom-call | tf_op jit(solution)/shard_map/solve/pallas_call | solution.py:433
  78.7 0.0 copy-start.2
  78.7 1.6 %copy.35 = f32[32,1024]{1,0:T(8,128)} copy(f32[32,1024]{1,0:T(8,128)} %get-tuple-element.6) | data formatting | bytes 262144
  80.3 0.0 copy-done.2
  80.3 0.7 copy.36
  (5 shorter events, 0.1 us)
Async XLA Ops:
  1.3 0.7 copy-start.7
  3.1 0.8 %copy-start.4 = (f32[128,128]{1,0:T(8,128)S(1)}, f32[128,128]{1,0:T(8,128)}, u32[]{:S(2)}) copy-start(f32[128,128]{1,0:T(8,128)} %param.10) | copy-start | bytes 196612
  4.0 0.8 %copy-start.5 = (f32[128,128]{1,0:T(8,128)S(1)}, f32[128,128]{1,0:T(8,128)}, u32[]{:S(2)}) copy-start(f32[128,128]{1,0:T(8,128)} %param.9) | copy-start | bytes 196612
  4.9 0.8 %copy-start.6 = (s32[128,128]{1,0:T(8,128)S(1)}, s32[128,128]{1,0:T(8,128)}, u32[]{:S(2)}) copy-start(s32[128,128]{1,0:T(8,128)} %param.12) | copy-start | bytes 196612
  7.2 34.1 %copy-start = (f32[32,1024]{1,0:T(8,128)S(1)}, f32[32,1024]{1,0:T(8,128)}, u32[]{:S(2)}) copy-start(f32[32,1024]{1,0:T(8,128)} %param.17) | copy-start | bytes 393220
  7.2 34.1 %copy-start.1 = (s32[32,1024]{1,0:T(8,128)S(1)}, s32[32,1024]{1,0:T(8,128)}, u32[]{:S(2)}) copy-start(s32[32,1024]{1,0:T(8,128)} %param.15) | copy-start | bytes 393220
  41.3 0.9 %copy-start.3 = (f32[32,1024]{1,0:T(8,128)S(1)}, f32[32,1024]{1,0:T(8,128)}, u32[]{:S(2)}) copy-start(f32[32,1024]{1,0:T(8,128)} %param.16) | copy-start | bytes 393220
  78.7 1.6 %copy-start.2 = (f32[32,1024]{1,0:T(8,128)S(1)}, f32[32,1024]{1,0:T(8,128)}, u32[]{:S(2)}) copy-start(f32[32,1024]{1,0:T(8,128)} %get-tuple-element.7) | copy-start | bytes 393220
